TPU v7x, 32 devices: a whole 2x2x4 slice. The times are simulated.
32 devices in a mesh: lat: 8 (over y, x, core), lon: 4 (over z).
Axes of the slice: x: 2, y: 2, z: 4, core: 2. Of those that a mesh axis runs over, the one named last changes fastest.
Arguments:
- fields: float32 [4, 6, 256, 1280], P(None, None, 'lat', 'lon'), may hold values from -6 to 6
- dep_row: int32 [6, 256, 1280], P(None, 'lat', 'lon'), may hold values from -4 to 255, as said below
- dep_col: int32 [6, 256, 1280], P(None, 'lat', 'lon'), may hold values from 0 to 1279, as said below
- weights: float32 [8, 6, 256, 1280], P(None, None, 'lat', 'lon'), may hold values from -0.25 to 0.75
Outputs:
- departed: float32 [4, 6, 256, 1280], P(None, None, 'lat', 'lon')
Inputs may be any that keep to these rules, and one draw needn't show every extreme that they name: dep_row[l, i, j] lies within i - 4 to i. dep_col[l, i, j] equals (j + k) modulo 1280 for some k from -4 to 0.
All inputs are finite; a program needn't handle non-finite values.
Results may differ from a plain program's by a relative error of at most 0.0003.
Values sent between devices are 32-bit elements; how exact they have to be, the bound alone decides.
A program may use at most 64 MiB of HBM per device.

v0:
```python
import jax
import jax.numpy as jnp
from jax import lax
from jax.sharding import PartitionSpec as P

HALO = 4


def padded_2(x, sides, width, wrap):
    for axis, dim in sides:
        devices, length = (lax.axis_size(axis), x.shape[dim])
        up = [(i, (i + 1) % devices) for i in range(devices if wrap else devices - 1)]
        down = [(j, i) for i, j in up]
        last = lax.slice_in_dim(x, length - width, length, axis=dim)
        leading = lax.slice_in_dim(x, 0, width, axis=dim)
        before = lax.ppermute(last, axis, up)
        after = lax.ppermute(leading, axis, down)
        x = jnp.concatenate([before, x, after], axis=dim)
    return x


def swapped(x, axis, stride):
    return lax.ppermute(x, axis, [(i, i ^ 1 << stride) for i in range(lax.axis_size(axis))])


def body(fields, dep_row, dep_col, weights):
    nfield, nlev, rows_here, cols_here = fields.shape
    lat_count = lax.axis_size("lat")
    lon_count = lax.axis_size("lon")
    band = lax.axis_index("lat")
    sector = lax.axis_index("lon")
    wide = padded_2(fields, (("lon", 3),), HALO, True)
    padded = padded_2(wide, (("lat", 2),), HALO, False)
    outgoing = jnp.where(band == 0, wide[:, :, :HALO], wide[:, :, rows_here - HALO :])
    partner = swapped(outgoing, "lon", lon_count.bit_length() - 2)
    flipped = partner[:, :, ::-1]
    north = jnp.where(band == 0, flipped, padded[:, :, :HALO])
    south = jnp.where(band == lat_count - 1, flipped, padded[:, :, rows_here + HALO :])
    padded = jnp.concatenate([north, padded[:, :, HALO : rows_here + HALO], south], axis=2)
    total_cols = cols_here * lon_count
    shape = (nlev, rows_here, cols_here)
    row_global = band * rows_here + lax.broadcasted_iota(jnp.int32, shape, 1)
    col_global = sector * cols_here + lax.broadcasted_iota(jnp.int32, shape, 2)
    offset_row = dep_row - row_global
    offset_col = jnp.mod(dep_col - col_global + HALO, total_cols) - HALO
    col_select = []
    row_select = []
    for shift in range(2 * HALO):
        col_term = jnp.zeros(shape, jnp.float32)
        row_term = jnp.zeros(shape, jnp.float32)
        for step in range(4):
            col_term = col_term + jnp.where(
                offset_col + step == shift - HALO, weights[4 + step], 0.0
            )
            row_term = row_term + jnp.where(offset_row + step == shift - HALO, weights[step], 0.0)
        col_select.append(col_term)
        row_select.append(row_term)
    total = jnp.zeros(fields.shape, jnp.float32)
    for row_shift in range(2 * HALO):
        band_rows = padded[:, :, row_shift : row_shift + rows_here]
        line = jnp.zeros(fields.shape, jnp.float32)
        for col_shift in range(2 * HALO):
            line = (
                line + col_select[col_shift] * band_rows[:, :, :, col_shift : col_shift + cols_here]
            )
        total = total + row_select[row_shift] * line
    return total


def solution(mesh):
    return jax.shard_map(
        body,
        mesh=mesh,
        in_specs=(
            P(None, None, "lat", "lon"),
            P(None, "lat", "lon"),
            P(None, "lat", "lon"),
            P(None, None, "lat", "lon"),
        ),
        out_specs=P(None, None, "lat", "lon"),
        check_vma=False,
    )
```

profile of v0, /device:TPU:3, one launch (start us, length us, event | category | flops | bytes accessed | tf_op | source)
XLA Modules:
  0.0 63.1 jit_solution(10448569810515244594)
XLA Ops:
  0.0 0.0 copy-start.4
  0.0 2.2 %fusion.131 = (f32[4,6,32,4]{3,2,1,0:T(8,128)}, f32[4,6,32,4]{3,2,1,0:T(8,128)}) fusion(f32[4,6,32,320]{3,2,1,0:T(8,128)} %param.4), kind=kLoop, calls=%fused_computation.271 | loop fusion | bytes 49152 | tf_op jit(solution)/shard_map/slice | solution.py:14
  2.2 1.3 %collective-permute-start = (f32[4,6,32,4]{3,2,1,0:T(8,128)}, f32[4,6,32,4]{3,2,1,0:T(8,128)}, u32[]{:S(2)}, u32[]{:S(2)}) collective-permute-start(f32[4,6,32,4]{3,2,1,0:T(8,128)} %get-tuple-element.26), channel_id=1, source_target_pairs={{0,1},{1,2},{2,3},{3,0},{4,5},{5,6},{6,7},{7,4},{8,9},{9,10},{10,1... | collective-permute-start | bytes 36872 | tf_op jit(solution)/shard_map/ppermute | solution.py:16
  3.5 2.0 %collective-permute-start.1 = (f32[4,6,32,4]{3,2,1,0:T(8,128)}, f32[4,6,32,4]{3,2,1,0:T(8,128)}, u32[]{:S(2)}, u32[]{:S(2)}) collective-permute-start(f32[4,6,32,4]{3,2,1,0:T(8,128)} %get-tuple-element.27), channel_id=1, source_target_pairs={{1,0},{2,1},{3,2},{0,3},{5,4},{6,5},{7,6},{4,7},{9,8},{10,9},{11,1... | collective-permute-start | bytes 36872 | tf_op jit(solution)/shard_map/ppermute | solution.py:17
  5.5 0.0 copy-done.4
  5.5 0.0 copy-start.1
  5.5 3.1 %fusion.83 = (f32[6,32,320]{2,1,0:T(8,128)}, f32[6,32,320]{2,1,0:T(8,128)}, f32[6,32,320]{2,1,0:T(8,128)}, f32[6,32,320]{2,1,0:T(8,128)}) fusion(f32[8,6,32,320]{3,2,1,0:T(8,128)} %param.7, s32[6,32,320]{2,1,0:T(8,128)S(1)} %copy-done.4, s32[320]{0:T(512)S(1)} %iota_add_fusion), kind=kLoop, calls=%fused_computation.158 | loop fusion | flops 3440640 | bytes 2213120 | tf_op jit(solution)/shard_map/add | solution.py:52
  8.6 0.0 copy-done.1
  8.6 1.7 %fusion.84 = (f32[6,32,320]{2,1,0:T(8,128)}, f32[6,32,320]{2,1,0:T(8,128)}, f32[6,32,320]{2,1,0:T(8,128)}, f32[6,32,320]{2,1,0:T(8,128)}) fusion(f32[8,6,32,320]{3,2,1,0:T(8,128)S(1)} %copy-done.1, s32[6,32,320]{2,1,0:T(8,128)S(1)} %copy-done.4, s32[320]{0:T(512)S(1)} %iota_add_fusion), kind=kLoop, calls=%fused_computation.159 | loop fusion | flops 3440640 | bytes 2213120 | tf_op jit(solution)/shard_map/add | solution.py:52
  10.2 0.0 copy-start
  10.2 2.6 %fusion.108 = (f32[6,32,320]{2,1,0:T(8,128)}, f32[6,32,320]{2,1,0:T(8,128)}, f32[6,32,320]{2,1,0:T(8,128)}, f32[6,32,320]{2,1,0:T(8,128)}) fusion(f32[8,6,32,320]{3,2,1,0:T(8,128)S(1)} %copy-done.1, s32[6,32,320]{2,1,0:T(8,128)} %param.5, s32[32]{0:T(128)S(1)} %iota_add_fusion.1), kind=kLoop, calls=%fused_computation.215 | loop fusion | flops 2949120 | bytes 2211968 | tf_op jit(solution)/shard_map/add | solution.py:55
  12.8 0.0 copy-start.5
  12.8 1.6 %collective-permute-done = f32[4,6,32,4]{3,2,1,0:T(8,128)} collective-permute-done((f32[4,6,32,4]{3,2,1,0:T(8,128)}, f32[4,6,32,4]{3,2,1,0:T(8,128)}, u32[]{:S(2)}, u32[]{:S(2)}) %collective-permute-start) | collective-permute-done | bytes 12320 | tf_op jit(solution)/shard_map/ppermute | solution.py:16
  14.4 8.2 %collective-permute-done.1 = f32[4,6,32,4]{3,2,1,0:T(8,128)} collective-permute-done((f32[4,6,32,4]{3,2,1,0:T(8,128)}, f32[4,6,32,4]{3,2,1,0:T(8,128)}, u32[]{:S(2)}, u32[]{:S(2)}) %collective-permute-start.1) | collective-permute-done | bytes 12320 | tf_op jit(solution)/shard_map/ppermute | solution.py:17
  22.7 0.0 copy-done
  22.7 2.1 %broadcast_select_fusion.2 = (f32[4,6,4,328]{3,2,1,0:T(4,128)}, f32[4,6,4,328]{3,2,1,0:T(4,128)}, f32[4,6,4,328]{3,2,1,0:T(4,128)}) fusion(pred[]{:T(512)S(6)} %eq.209, f32[4,6,32,4]{3,2,1,0:T(8,128)} %collective-permute-done.1, f32[4,6,32,320]{3,2,1,0:T(8,128)S(1)} %copy-done, f32[4,6,32,4]{3,2,1,0:T(8,128)} %collective-permute-done), kind=kLoop, calls=%fused_computation.268 | loop fusion | flops 157440 | bytes 1385473 | tf_op jit(solution)/shard_map/jit(_where)/select_n | solution.py:34
  24.7 0.5 collective-permute-start.2
  25.2 4.9 %collective-permute-start.3 = (f32[4,6,4,328]{3,2,1,0:T(4,128)}, f32[4,6,4,328]{3,2,1,0:T(4,128)S(1)}, u32[]{:S(2)}, u32[]{:S(2)}) collective-permute-start(f32[4,6,4,328]{3,2,1,0:T(4,128)} %get-tuple-element.6), channel_id=1, source_target_pairs={{0,4},{4,8},{8,12},{12,16},{16,20},{20,24},{24,28},{1,5},{5,9},{9,... | collective-permute-start | bytes 377864 | tf_op jit(solution)/shard_map/ppermute | solution.py:16
  30.1 1.9 %collective-permute-start.4 = (f32[4,6,4,328]{3,2,1,0:T(4,128)}, f32[4,6,4,328]{3,2,1,0:T(4,128)S(1)}, u32[]{:S(2)}, u32[]{:S(2)}) collective-permute-start(f32[4,6,4,328]{3,2,1,0:T(4,128)} %get-tuple-element.7), channel_id=1, source_target_pairs={{4,0},{8,4},{12,8},{16,12},{20,16},{24,20},{28,24},{5,1},{9,5},{13... | collective-permute-start | bytes 377864 | tf_op jit(solution)/shard_map/ppermute | solution.py:17
  32.0 0.0 copy-done.5
  32.0 1.6 %fusion.107 = (f32[6,32,320]{2,1,0:T(8,128)}, f32[6,32,320]{2,1,0:T(8,128)}, f32[6,32,320]{2,1,0:T(8,128)}, f32[6,32,320]{2,1,0:T(8,128)}) fusion(f32[8,6,32,320]{3,2,1,0:T(8,128)S(1)} %copy-done.1, s32[6,32,320]{2,1,0:T(8,128)S(1)} %copy-done.5, s32[32]{0:T(128)S(1)} %iota_add_fusion.1), kind=kLoop, calls=%fused_computation.214 | loop fusion | flops 2949120 | bytes 2211968 | tf_op jit(solution)/shard_map/add | solution.py:55
  33.6 0.1 collective-permute-done.2
  33.7 0.3 rev.3
  33.9 0.0 collective-permute-done.3
  33.9 3.7 %collective-permute-done.4 = f32[4,6,4,328]{3,2,1,0:T(4,128)S(1)} collective-permute-done((f32[4,6,4,328]{3,2,1,0:T(4,128)}, f32[4,6,4,328]{3,2,1,0:T(4,128)S(1)}, u32[]{:S(2)}, u32[]{:S(2)}) %collective-permute-start.4) | collective-permute-done | bytes 125984 | tf_op jit(solution)/shard_map/ppermute | solution.py:17
  37.7 0.0 copy-start.2
  37.7 0.0 copy-start.3
  37.7 3.1 %maximum_maximum_fusion = (f32[4,6,36,328]{3,2,1,0:T(8,128)S(1)}, f32[4,6,36,328]{3,2,1,0:T(8,128)S(1)}) fusion(f32[4,6,32,4]{3,2,1,0:T(8,128)} %collective-permute-done.1, f32[4,6,32,320]{3,2,1,0:T(8,128)} %param.4, f32[4,6,32,4]{3,2,1,0:T(8,128)} %collective-permute-done, f32[4,6,4,328]{3,2,1,0:T(4,128)S(1)} %bitcast.269, f32[4,6,4,328]{3,2,1,0:T(4,128)S(1)} %bitcast.270), kind=kLoop, calls=%fused_computation.5 | loop fusion | flops 1700352 | bytes 3526656 | tf_op jit(solution)/shard_map/concatenate | solution.py:39
  40.8 0.0 copy-done.2
  40.9 0.0 copy-done.3
  40.9 22.3 %fusion.8 = f32[4,6,32,320]{3,2,1,0:T(8,128)} fusion(f32[4,6,32,4]{3,2,1,0:T(8,128)} %collective-permute-done.1, f32[4,6,32,4]{3,2,1,0:T(8,128)} %collective-permute-done, f32[4,6,36,328]{3,2,1,0:T(8,128)S(1)} %get-tuple-element.25, f32[4,6,32,320]{3,2,1,0:T(8,128)} %param.4, f32[4,6,36,328]{3,2,1,0:T(8,128)S(1)} %get-tuple-element.24, ...), kind=kLoop, calls=%fused_computation.15 | loop fusion | flops 34897920 | bytes 60973056 | tf_op jit(solution)/shard_map/add | solution.py:66
  (3 shorter events, 0.0 us)
Async XLA Ops:
  0.0 5.5 %copy-start.4 = (s32[6,32,320]{2,1,0:T(8,128)S(1)}, s32[6,32,320]{2,1,0:T(8,128)}, u32[]{:S(2)}) copy-start(s32[6,32,320]{2,1,0:T(8,128)} %param.6) | copy-start | bytes 737284
  2.2 12.3 %collective-permute-start = (f32[4,6,32,4]{3,2,1,0:T(8,128)}, f32[4,6,32,4]{3,2,1,0:T(8,128)}, u32[]{:S(2)}, u32[]{:S(2)}) collective-permute-start(f32[4,6,32,4]{3,2,1,0:T(8,128)} %get-tuple-element.26), channel_id=1, source_target_pairs={{0,1},{1,2},{2,3},{3,0},{4,5},{5,6},{6,7},{7,4},{8,9},{9,10},{10,1... | collective-permute-start | bytes 36872 | tf_op jit(solution)/shard_map/ppermute | solution.py:16
  3.5 19.2 %collective-permute-start.1 = (f32[4,6,32,4]{3,2,1,0:T(8,128)}, f32[4,6,32,4]{3,2,1,0:T(8,128)}, u32[]{:S(2)}, u32[]{:S(2)}) collective-permute-start(f32[4,6,32,4]{3,2,1,0:T(8,128)} %get-tuple-element.27), channel_id=1, source_target_pairs={{1,0},{2,1},{3,2},{0,3},{5,4},{6,5},{7,6},{4,7},{9,8},{10,9},{11,1... | collective-permute-start | bytes 36872 | tf_op jit(solution)/shard_map/ppermute | solution.py:17
  5.5 3.1 %copy-start.1 = (f32[8,6,32,320]{3,2,1,0:T(8,128)S(1)}, f32[8,6,32,320]{3,2,1,0:T(8,128)}, u32[]{:S(2)}) copy-start(f32[8,6,32,320]{3,2,1,0:T(8,128)} %param.7) | copy-start | bytes 5898244
  10.2 12.4 %copy-start = (f32[4,6,32,320]{3,2,1,0:T(8,128)S(1)}, f32[4,6,32,320]{3,2,1,0:T(8,128)}, u32[]{:S(2)}) copy-start(f32[4,6,32,320]{3,2,1,0:T(8,128)} %param.4) | copy-start | bytes 2949124
  12.8 19.2 %copy-start.5 = (s32[6,32,320]{2,1,0:T(8,128)S(1)}, s32[6,32,320]{2,1,0:T(8,128)}, u32[]{:S(2)}) copy-start(s32[6,32,320]{2,1,0:T(8,128)} %param.5) | copy-start | bytes 737284
  24.7 8.9 %collective-permute-start.2 = (f32[4,6,4,328]{3,2,1,0:T(4,128)}, f32[4,6,4,328]{3,2,1,0:T(4,128)S(1)}, u32[]{:S(2)}, u32[]{:S(2)}) collective-permute-start(f32[4,6,4,328]{3,2,1,0:T(4,128)} %get-tuple-element.5), channel_id=1, source_target_pairs={{0,2},{1,3},{2,0},{3,1},{4,6},{5,7},{6,4},{7,5},{8,10},{9,11},{10,... | collective-permute-start | bytes 377864 | tf_op jit(solution)/shard_map/ppermute | solution.py:23
  25.2 8.7 %collective-permute-start.3 = (f32[4,6,4,328]{3,2,1,0:T(4,128)}, f32[4,6,4,328]{3,2,1,0:T(4,128)S(1)}, u32[]{:S(2)}, u32[]{:S(2)}) collective-permute-start(f32[4,6,4,328]{3,2,1,0:T(4,128)} %get-tuple-element.6), channel_id=1, source_target_pairs={{0,4},{4,8},{8,12},{12,16},{16,20},{20,24},{24,28},{1,5},{5,9},{9,... | collective-permute-start | bytes 377864 | tf_op jit(solution)/shard_map/ppermute | solution.py:16
  30.1 7.6 %collective-permute-start.4 = (f32[4,6,4,328]{3,2,1,0:T(4,128)}, f32[4,6,4,328]{3,2,1,0:T(4,128)S(1)}, u32[]{:S(2)}, u32[]{:S(2)}) collective-permute-start(f32[4,6,4,328]{3,2,1,0:T(4,128)} %get-tuple-element.7), channel_id=1, source_target_pairs={{4,0},{8,4},{12,8},{16,12},{20,16},{24,20},{28,24},{5,1},{9,5},{13... | collective-permute-start | bytes 377864 | tf_op jit(solution)/shard_map/ppermute | solution.py:17
  37.7 3.1 %copy-start.2 = (f32[6,32,320]{2,1,0:T(8,128)S(1)}, f32[6,32,320]{2,1,0:T(8,128)}, u32[]{:S(2)}) copy-start(f32[6,32,320]{2,1,0:T(8,128)} %get-tuple-element.8) | copy-start | bytes 737284
  37.7 3.1 %copy-start.3 = (f32[6,32,320]{2,1,0:T(8,128)S(1)}, f32[6,32,320]{2,1,0:T(8,128)}, u32[]{:S(2)}) copy-start(f32[6,32,320]{2,1,0:T(8,128)} %get-tuple-element.9) | copy-start | bytes 737284
where the time goes:
time: 63.4 us; the launch traced here: 63.1 us
  other arithmetic  36.4 us (57%)
  waiting for transfers between devices  13.6 us (21%)
  starting transfers between devices  10.6 us (17%)
  local copies, waits for them, and re-layouts  2.45 us (4%)
    add x1, other arithmetic, body(): total = total + row_select[row_shift] * line  22.3 us
    ppermute x2, waiting for transfers between devices, padded_2(): after = lax.ppermute(leading, axis, down)  12 us
    ppermute x2, starting transfers between devices, padded_2(): before = lax.ppermute(last, axis, up)  6.17 us
    add x2, other arithmetic, body(): col_term + jnp.where(offset_col + step == shift - HALO, weights[4 + step]...  4.73 us
    add x2, other arithmetic, body(): row_term + jnp.where(offset_row + step == shift - HALO, weights[step], 0.0)  4.18 us
    ppermute x2, starting transfers between devices, padded_2(): after = lax.ppermute(leading, axis, down)  3.95 us
    concatenate x1, other arithmetic, body(): jnp.concatenate([north, padded[:, :, HALO:rows_here + HALO], south], axis=2)  3.11 us
    slice x1, local copies, waits for them, and re-layouts, padded_2(): last = lax.slice_in_dim(x, length - width, length, axis=dim)  2.16 us
  transfers between devices with their start and end apart: 5, of which 4 were waited for; matrix products, arithmetic and copies ran while one was open for 15% of the time, Pallas kernels for 0%

commit v1 on v0

v1 whole, which is shorter than its diff:
```python
import functools

import jax
import jax.numpy as jnp
from jax import lax
from jax.experimental import pallas as pl
from jax.experimental.pallas import tpu as pltpu
from jax.sharding import PartitionSpec as P

HALO = 4
LANES = 128
SUB = 8
CHUNK = LANES - 2 * HALO
NSHIFT = 2 * HALO


def beside(x, axis, dim, width, wrap):
    devices, length = (lax.axis_size(axis), x.shape[dim])
    up = [(i, (i + 1) % devices) for i in range(devices if wrap else devices - 1)]
    down = [(j, i) for i, j in up]
    last = lax.slice_in_dim(x, length - width, length, axis=dim)
    leading = lax.slice_in_dim(x, 0, width, axis=dim)
    return lax.ppermute(last, axis, up), lax.ppermute(leading, axis, down)


def swapped(x, axis, stride):
    return lax.ppermute(x, axis, [(i, i ^ 1 << stride) for i in range(lax.axis_size(axis))])


def lane_index():
    return lax.broadcasted_iota(jnp.int32, (SUB, LANES), 1)


def chunked(tiles, side=None):
    lane = lane_index()
    out = [tiles[0] if side is None else jnp.where(lane < LANES - HALO, tiles[0], side)]
    for t in range(1, len(tiles)):
        back = (LANES - CHUNK) * t
        mixed = jnp.where(lane < LANES - HALO - back, tiles[t], tiles[t - 1])
        out.append(pltpu.roll(mixed, back, 1))
    return out


def unchunked(chunks):
    lane = lane_index()
    count = len(chunks)
    ahead = [c if t == 0 else pltpu.roll(c, LANES - (LANES - CHUNK) * t, 1) for t, c in enumerate(chunks)]
    return [
        ahead[t] if t == count - 1 else jnp.where(lane < CHUNK - (LANES - CHUNK) * t, ahead[t], ahead[t + 1])
        for t in range(count)
    ]


def spread(offset, w):
    one, two, four = (offset & 1) != 0, (offset & 2) != 0, offset == 4
    zero = jnp.zeros_like(w[0])
    u = [jnp.where(one, a, b) for a, b in zip([zero] + w, w + [zero])]
    v = [jnp.where(two, a, b) for a, b in zip([zero, zero] + u, u + [zero, zero])]
    return [jnp.where(four, a, b) for a, b in zip([zero] * 4 + w, v + [zero])]


def stencil(cols, total_cols, fields_ref, row_ref, col_ref, weight_ref, side_ref, caps_ref, out_ref, xs, sel, res):
    nfield, rows = fields_ref.shape[0], fields_ref.shape[2]
    tiles = pl.cdiv(cols, LANES)
    groups = rows // SUB
    row0 = lax.axis_index("lat") * rows
    col0 = lax.axis_index("lon") * cols
    lane = lane_index()
    sub = lax.broadcasted_iota(jnp.int32, (SUB, LANES), 0)
    lanes_of = [pl.ds(LANES * t, LANES) for t in range(tiles)]

    for i in range(groups):
        span = pl.ds(SUB * i, SUB)
        offsets = []
        for t in range(tiles):
            o_row = row_ref[0, span, lanes_of[t]] - (row0 + SUB * i + sub) + HALO
            back = col_ref[0, span, lanes_of[t]] - (col0 + LANES * t + lane)
            o_col = jnp.where(back > 0, back - total_cols, back) + HALO
            offsets.append(o_row * 16 + o_col)
        offsets = chunked(offsets)
        w = [chunked([weight_ref[q, 0, span, at] for at in lanes_of]) for q in range(8)]
        for t in range(tiles):
            for base, offset in ((0, offsets[t] >> 4), (4, offsets[t] & 15)):
                slots = spread(offset, [w[base + a][t] for a in range(4)])
                for s in range(NSHIFT):
                    sel[2 * base + s, t, span, :] = slots[s]

    for f in range(nfield):
        for i in range(groups):
            span = pl.ds(SUB * i, SUB)
            side = side_ref[f, 0, span, :]
            got = [fields_ref[f, 0, span, at] for at in lanes_of]
            got[-1] = jnp.where(lane < cols - LANES * (tiles - 1), got[-1], side)
            for t, chunk in enumerate(chunked(got, side)):
                xs[f, t, pl.ds(SUB * (i + 1), SUB), :] = chunk
        got = [caps_ref[f, 0, :, at] for at in lanes_of]
        for t, chunk in enumerate(chunked(got, got[-1])):
            xs[f, t, pl.ds(0, SUB), :] = chunk
            xs[f, t, pl.ds(SUB * (groups + 1), SUB), :] = chunk

    stride = rows // SUB
    many = 2 if stride % 2 == 0 else 1
    pair = 2 if nfield % 2 == 0 else 1
    for t in range(tiles):
        for m0 in range(0, stride, many):
            rowsel = [
                [sel[r, t, pl.ds(m0 + m, SUB, stride=stride), :] for r in range(NSHIFT)] for m in range(many)
            ]
            for f0 in range(0, nfield, pair):
                total = [[None] * pair for _ in range(many)]
                for s in range(NSHIFT):
                    colsel = [sel[NSHIFT + s, t, pl.ds(m0 + m, SUB, stride=stride), :] for m in range(many)]
                    for f in range(pair):
                        x = []
                        for r in range(many + NSHIFT - 1):
                            value = xs[f0 + f, t, pl.ds(HALO + m0 + r, SUB, stride=stride), :]
                            x.append(value if s == HALO else pltpu.roll(value, (HALO - s) % LANES, 1))
                        for m in range(many):
                            line = rowsel[m][0] * x[m]
                            for r in range(1, NSHIFT):
                                line = line + rowsel[m][r] * x[m + r]
                            term = colsel[m] * line
                            total[m][f] = term if s == 0 else total[m][f] + term
                for m in range(many):
                    for f in range(pair):
                        res[f0 + f, t, pl.ds(m0 + m, SUB, stride=stride), :] = total[m][f]
    for f in range(nfield):
        for i in range(groups):
            span = pl.ds(SUB * i, SUB)
            for t, tile in enumerate(unchunked([res[f, t, span, :] for t in range(tiles)])):
                out_ref[f, 0, span, lanes_of[t]] = tile


def halos(fields):
    nfield, nlev, rows, cols = fields.shape
    band, lat_count, lon_count = lax.axis_index("lat"), lax.axis_size("lat"), lax.axis_size("lon")
    west, east = beside(fields, "lon", 3, HALO, True)
    wide = jnp.concatenate([west, fields, east], axis=3)
    from_north, from_south = beside(wide, "lat", 2, HALO, False)
    outgoing = jnp.where(band == 0, wide[:, :, :HALO], wide[:, :, rows - HALO :])
    flipped = swapped(outgoing, "lon", lon_count.bit_length() - 2)[:, :, ::-1]
    north = jnp.where(band == 0, flipped, from_north)
    south = jnp.where(band == lat_count - 1, flipped, from_south)
    last = LANES * ((cols - 1) // LANES)

    def gap(h, n):
        return jnp.zeros((nfield, nlev, h, n), jnp.float32)

    tail = last + LANES - cols - 2 * HALO
    side = jnp.concatenate([gap(rows, cols - last), east, gap(rows, tail), west], axis=3)
    caps = jnp.concatenate([south, north], axis=2)
    caps = jnp.concatenate([caps[..., HALO:], gap(2 * HALO, tail), caps[..., :HALO]], axis=3)
    return side, caps


def body(fields, dep_row, dep_col, weights):
    nfield, nlev, rows, cols = fields.shape
    side, caps = halos(fields)
    tiles = pl.cdiv(cols, LANES)
    wide = tiles * LANES
    assert rows % SUB == 0 and CHUNK * tiles >= cols and cols + 2 * HALO <= wide

    def block(lead, h, w):
        return pl.BlockSpec((lead, 1, h, w), lambda l: (0, l, 0, 0))

    point = pl.BlockSpec((1, rows, wide), lambda l: (l, 0, 0))
    return pl.pallas_call(
        functools.partial(stencil, cols, cols * lax.axis_size("lon")),
        grid=(nlev,),
        out_shape=jax.ShapeDtypeStruct(fields.shape, jnp.float32),
        in_specs=[
            block(nfield, rows, wide),
            point,
            point,
            block(8, rows, wide),
            block(nfield, rows, LANES),
            block(nfield, 2 * HALO, wide),
        ],
        out_specs=block(nfield, rows, wide),
        scratch_shapes=[
            pltpu.VMEM((nfield, tiles, rows + 2 * SUB, LANES), jnp.float32),
            pltpu.VMEM((2 * NSHIFT, tiles, rows, LANES), jnp.float32),
            pltpu.VMEM((nfield, tiles, rows, LANES), jnp.float32),
        ],
    )(fields, dep_row, dep_col, weights, side, caps)


def solution(mesh):
    return jax.shard_map(
        body,
        mesh=mesh,
        in_specs=(
            P(None, None, "lat", "lon"),
            P(None, "lat", "lon"),
            P(None, "lat", "lon"),
            P(None, None, "lat", "lon"),
        ),
        out_specs=P(None, None, "lat", "lon"),
        check_vma=False,
    )
```

time: 63.4 us -> 50.5 us (0.80)
  other arithmetic: 36.4 us -> 2.37 us
  Pallas kernels: 0 us -> 14.4 us
  waiting for transfers between devices: 13.6 us -> 21.1 us
    add x7 -> x0, other arithmetic: 31.2 us -> none  [the longest x1 22.3 us: body(): total = total + row_select[row_shift] * line]
    pallas_call x0 -> x1, Pallas kernels: none -> 14.4 us  [body(): pl.pallas_call(functools.partial(stencil, cols, cols * lax.axis_size('lon...]
    ppermute x4, waiting for transfers between devices: 13.6 us -> 20.6 us  [beside(): return (lax.ppermute(last, axis, up), lax.ppermute(leading, axis, down))]
    select_n x2, other arithmetic: 2.1 us -> 0.3 us  [the longest x1 0.27 us: halos(): outgoing = jnp.where(band == 0, wide[:, :, :HALO], wide[:, :, rows - HALO:])]
    concatenate x1 -> x3, other arithmetic: 3.11 us -> 2.07 us  [the longest x1 1.01 us: halos(): jnp.concatenate([gap(rows, cols - last), east, gap(rows, tail), west], ax...]
    slice x1, local copies, waits for them, and re-layouts: 2.16 us -> 1.39 us  [beside(): leading = lax.slice_in_dim(x, 0, width, axis=dim)]
  transfers between devices with their start and end apart: 5 -> 5, of which waited for: 4 -> 4; matrix products, arithmetic and copies ran while one was open for 15% -> 3% of each run, Pallas kernels for 0% -> 0%
where the time goes in v1:
time: 50.5 us; the launch traced here: 50.3 us
  waiting for transfers between devices  21.1 us (42%)
  Pallas kernels  14.4 us (29%)
  starting transfers between devices  10.6 us (21%)
  other arithmetic  2.37 us (5%)
  local copies, waits for them, and re-layouts  1.82 us (4%)
    ppermute x4, waiting for transfers between devices, beside(): return (lax.ppermute(last, axis, up), lax.ppermute(leading, axis, down))  20.6 us
    pallas_call x1, Pallas kernels, body(): pl.pallas_call(functools.partial(stencil, cols, cols * lax.axis_size('lon...  14.4 us
    ppermute x4, starting transfers between devices, beside(): return (lax.ppermute(last, axis, up), lax.ppermute(leading, axis, down))  10.4 us
    slice x1, local copies, waits for them, and re-layouts, beside(): leading = lax.slice_in_dim(x, 0, width, axis=dim)  1.39 us
    concatenate x1, other arithmetic, halos(): jnp.concatenate([gap(rows, cols - last), east, gap(rows, tail), west], ax...  1.01 us
  transfers between devices with their start and end apart: 5, of which 4 were waited for; matrix products, arithmetic and copies ran while one was open for 3% of the time, Pallas kernels for 0%

profile of v1, /device:TPU:3, one launch (start us, length us, event | category | flops | bytes accessed | tf_op | source)
XLA Modules:
  0.0 50.3 jit_solution(17917537195651644999)
XLA Ops:
  0.0 0.0 copy-start
  0.0 1.4 %fusion.1 = (f32[4,6,32,4]{3,2,1,0:T(8,128)S(1)}, f32[4,6,32,4]{3,2,1,0:T(8,128)S(1)}) fusion(f32[4,6,32,320]{3,2,1,0:T(8,128)} %fields_ref.1), kind=kLoop, calls=%fused_computation.10 | loop fusion | bytes 49152 | tf_op jit(solution)/shard_map/slice | solution.py:22
  1.4 3.4 %collective-permute-start = (f32[4,6,32,4]{3,2,1,0:T(8,128)S(1)}, f32[4,6,32,4]{3,2,1,0:T(8,128)S(1)}, u32[]{:S(2)}, u32[]{:S(2)}) collective-permute-start(f32[4,6,32,4]{3,2,1,0:T(8,128)S(1)} %get-tuple-element.8), channel_id=1, source_target_pairs={{1,0},{2,1},{3,2},{0,3},{5,4},{6,5},{7,6},{4,7},{9,8},{10,9},{11,1... | collective-permute-start | bytes 36872 | tf_op jit(solution)/shard_map/ppermute | solution.py:23
  4.8 0.0 collective-permute-start.1
  4.8 0.1 pad.10.clone
  4.8 0.1 pad.1.clone
  4.9 7.7 %collective-permute-done = f32[4,6,32,4]{3,2,1,0:T(8,128)S(1)} collective-permute-done((f32[4,6,32,4]{3,2,1,0:T(8,128)S(1)}, f32[4,6,32,4]{3,2,1,0:T(8,128)S(1)}, u32[]{:S(2)}, u32[]{:S(2)}) %collective-permute-start) | collective-permute-done | bytes 12320 | tf_op jit(solution)/shard_map/ppermute | solution.py:23
  12.7 9.2 %collective-permute-done.1 = f32[4,6,32,4]{3,2,1,0:T(8,128)S(1)} collective-permute-done((f32[4,6,32,4]{3,2,1,0:T(8,128)S(1)}, f32[4,6,32,4]{3,2,1,0:T(8,128)S(1)}, u32[]{:S(2)}, u32[]{:S(2)}) %collective-permute-start.1) | collective-permute-done | bytes 12320 | tf_op jit(solution)/shard_map/ppermute | solution.py:23
  21.9 0.0 copy-done
  21.9 0.3 broadcast_select_fusion.1
  22.2 0.2 collective-permute-start.2
  22.4 5.1 %collective-permute-start.4 = (f32[4,6,4,328]{3,2,1,0:T(4,128)S(1)}, f32[4,6,4,328]{3,2,1,0:T(4,128)S(1)}, u32[]{:S(2)}, u32[]{:S(2)}) collective-permute-start(f32[4,6,4,328]{3,2,1,0:T(4,128)S(1)} %get-tuple-element.6), channel_id=1, source_target_pairs={{0,4},{4,8},{8,12},{12,16},{16,20},{20,24},{24,28},{1,5},{5,9},{9,... | collective-permute-start | bytes 377864 | tf_op jit(solution)/shard_map/ppermute | solution.py:23
  27.5 1.9 %collective-permute-start.3 = (f32[4,6,4,328]{3,2,1,0:T(4,128)S(1)}, f32[4,6,4,328]{3,2,1,0:T(4,128)S(1)}, u32[]{:S(2)}, u32[]{:S(2)}) collective-permute-start(f32[4,6,4,328]{3,2,1,0:T(4,128)S(1)} %get-tuple-element.7), channel_id=1, source_target_pairs={{4,0},{8,4},{12,8},{16,12},{20,16},{24,20},{28,24},{5,1},{9,5},{13... | collective-permute-start | bytes 377864 | tf_op jit(solution)/shard_map/ppermute | solution.py:23
  29.4 1.0 %pad_maximum_fusion.side_ref = f32[4,6,32,128]{3,2,1,0:T(8,128)} fusion(f32[4,6,32,4]{3,2,1,0:T(8,128)S(1)} %collective-permute-done.1, f32[4,6,32,4]{3,2,1,0:T(8,128)S(1)} %collective-permute-done, f32[128]{0:T(128)S(1)} %pad.10.clone, f32[128]{0:T(128)S(1)} %pad.8.clone), kind=kLoop, calls=%fused_computation | loop fusion | flops 294912 | bytes 418816 | tf_op jit(solution)/shard_map/concatenate | solution.py:150
  30.4 0.5 %collective-permute-done.2 = f32[4,6,4,328]{3,2,1,0:T(4,128)S(1)} collective-permute-done((f32[4,6,4,328]{3,2,1,0:T(4,128)S(1)}, f32[4,6,4,328]{3,2,1,0:T(4,128)S(1)}, u32[]{:S(2)}, u32[]{:S(2)}) %collective-permute-start.2) | collective-permute-done | bytes 125984 | tf_op jit(solution)/shard_map/ppermute | solution.py:27
  31.0 0.3 rev.3
  31.2 0.0 collective-permute-done.4
  31.2 3.6 %collective-permute-done.3 = f32[4,6,4,328]{3,2,1,0:T(4,128)S(1)} collective-permute-done((f32[4,6,4,328]{3,2,1,0:T(4,128)S(1)}, f32[4,6,4,328]{3,2,1,0:T(4,128)S(1)}, u32[]{:S(2)}, u32[]{:S(2)}) %collective-permute-start.3) | collective-permute-done | bytes 125984 | tf_op jit(solution)/shard_map/ppermute | solution.py:23
  34.9 0.2 slice_maximum_fusion
  35.1 0.8 %fusion.caps_ref = f32[4,6,8,384]{3,2,1,0:T(8,128)} fusion(f32[4,6,4,328]{3,2,1,0:T(4,128)S(1)} %bitcast.8, f32[4,6,4,328]{3,2,1,0:T(4,128)S(1)} %bitcast.6, f32[4,6,8,324]{3,2,1,0:T(8,128)S(1)} %slice_maximum_fusion, f32[384]{0:T(512)S(1)} %pad.1.clone), kind=kLoop, calls=%fused_computation.2 | loop fusion | flops 221184 | bytes 797184 | tf_op jit(solution)/shard_map/concatenate | solution.py:152
  36.0 14.4 %shard_map.46 = f32[4,6,32,320]{3,2,1,0:T(8,128)} custom-call(f32[4,6,32,320]{3,2,1,0:T(8,128)} %fields_ref.1, s32[6,32,320]{2,1,0:T(8,128)} %row_ref.1, s32[6,32,320]{2,1,0:T(8,128)} %col_ref.1, f32[8,6,32,320]{3,2,1,0:T(8,128)} %weight_ref.1, f32[4,6,32,128]{3,2,1,0:T(8,128)} %pad_maximum_fusion.side_ref, f32[4,6,8,384]{3,2,1,0:T(8,128)} %fusion.caps_ref), custom_call_target="tpu_custom_call" | custom-call | tf_op jit(solution)/shard_map/pallas_call | solution.py:167
  (4 shorter events, 0.0 us)
Async XLA Ops:
  0.0 21.9 %copy-start = (f32[4,6,32,320]{3,2,1,0:T(8,128)S(1)}, f32[4,6,32,320]{3,2,1,0:T(8,128)}, u32[]{:S(2)}) copy-start(f32[4,6,32,320]{3,2,1,0:T(8,128)} %fields_ref.1) | copy-start | bytes 2949124
  1.4 11.3 %collective-permute-start = (f32[4,6,32,4]{3,2,1,0:T(8,128)S(1)}, f32[4,6,32,4]{3,2,1,0:T(8,128)S(1)}, u32[]{:S(2)}, u32[]{:S(2)}) collective-permute-start(f32[4,6,32,4]{3,2,1,0:T(8,128)S(1)} %get-tuple-element.8), channel_id=1, source_target_pairs={{1,0},{2,1},{3,2},{0,3},{5,4},{6,5},{7,6},{4,7},{9,8},{10,9},{11,1... | collective-permute-start | bytes 36872 | tf_op jit(solution)/shard_map/ppermute | solution.py:23
  4.8 17.1 %collective-permute-start.1 = (f32[4,6,32,4]{3,2,1,0:T(8,128)S(1)}, f32[4,6,32,4]{3,2,1,0:T(8,128)S(1)}, u32[]{:S(2)}, u32[]{:S(2)}) collective-permute-start(f32[4,6,32,4]{3,2,1,0:T(8,128)S(1)} %get-tuple-element.9), channel_id=1, source_target_pairs={{0,1},{1,2},{2,3},{3,0},{4,5},{5,6},{6,7},{7,4},{8,9},{9,10},{10,1... | collective-permute-start | bytes 36872 | tf_op jit(solution)/shard_map/ppermute | solution.py:23
  22.2 8.8 %collective-permute-start.2 = (f32[4,6,4,328]{3,2,1,0:T(4,128)S(1)}, f32[4,6,4,328]{3,2,1,0:T(4,128)S(1)}, u32[]{:S(2)}, u32[]{:S(2)}) collective-permute-start(f32[4,6,4,328]{3,2,1,0:T(4,128)S(1)} %get-tuple-element.5), channel_id=1, source_target_pairs={{0,2},{1,3},{2,0},{3,1},{4,6},{5,7},{6,4},{7,5},{8,10},{9,11},{10,... | collective-permute-start | bytes 377864 | tf_op jit(solution)/shard_map/ppermute | solution.py:27
  22.4 8.8 %collective-permute-start.4 = (f32[4,6,4,328]{3,2,1,0:T(4,128)S(1)}, f32[4,6,4,328]{3,2,1,0:T(4,128)S(1)}, u32[]{:S(2)}, u32[]{:S(2)}) collective-permute-start(f32[4,6,4,328]{3,2,1,0:T(4,128)S(1)} %get-tuple-element.6), channel_id=1, source_target_pairs={{0,4},{4,8},{8,12},{12,16},{16,20},{20,24},{24,28},{1,5},{5,9},{9,... | collective-permute-start | bytes 377864 | tf_op jit(solution)/shard_map/ppermute | solution.py:23
  27.5 7.4 %collective-permute-start.3 = (f32[4,6,4,328]{3,2,1,0:T(4,128)S(1)}, f32[4,6,4,328]{3,2,1,0:T(4,128)S(1)}, u32[]{:S(2)}, u32[]{:S(2)}) collective-permute-start(f32[4,6,4,328]{3,2,1,0:T(4,128)S(1)} %get-tuple-element.7), channel_id=1, source_target_pairs={{4,0},{8,4},{12,8},{16,12},{20,16},{24,20},{28,24},{5,1},{9,5},{13... | collective-permute-start | bytes 377864 | tf_op jit(solution)/shard_map/ppermute | solution.py:23

commit v2 on v1

--- a/solution.py
+++ b/solution.py
@@ -14,21 +14,12 @@
 NSHIFT = 2 * HALO
 
 
-def beside(x, axis, dim, width, wrap):
-    devices, length = (lax.axis_size(axis), x.shape[dim])
-    up = [(i, (i + 1) % devices) for i in range(devices if wrap else devices - 1)]
-    down = [(j, i) for i, j in up]
-    last = lax.slice_in_dim(x, length - width, length, axis=dim)
-    leading = lax.slice_in_dim(x, 0, width, axis=dim)
-    return lax.ppermute(last, axis, up), lax.ppermute(leading, axis, down)
-
-
-def swapped(x, axis, stride):
-    return lax.ppermute(x, axis, [(i, i ^ 1 << stride) for i in range(lax.axis_size(axis))])
-
-
 def lane_index():
     return lax.broadcasted_iota(jnp.int32, (SUB, LANES), 1)
+
+
+def sublane_index():
+    return lax.broadcasted_iota(jnp.int32, (SUB, LANES), 0)
 
 
 def chunked(tiles, side=None):
@@ -59,14 +50,17 @@
     return [jnp.where(four, a, b) for a, b in zip([zero] * 4 + w, v + [zero])]
 
 
-def stencil(cols, total_cols, fields_ref, row_ref, col_ref, weight_ref, side_ref, caps_ref, out_ref, xs, sel, res):
+def stencil(cols, total_cols, fields_ref, row_ref, col_ref, weight_ref, west_ref, east_ref, rows_ref, corner_ref, out_ref, xs, sel, res):
     nfield, rows = fields_ref.shape[0], fields_ref.shape[2]
     tiles = pl.cdiv(cols, LANES)
     groups = rows // SUB
     row0 = lax.axis_index("lat") * rows
     col0 = lax.axis_index("lon") * cols
-    lane = lane_index()
-    sub = lax.broadcasted_iota(jnp.int32, (SUB, LANES), 0)
+    level = pl.program_id(0)
+    held = cols - LANES * (tiles - 1)
+    lane, sub = lane_index(), sublane_index()
+    top, bottom = lax.axis_index("lat") == 0, lax.axis_index("lat") == lax.axis_size("lat") - 1
+    turned = ((sub < HALO) & bottom) | ((sub >= HALO) & top)
     lanes_of = [pl.ds(LANES * t, LANES) for t in range(tiles)]
 
     for i in range(groups):
@@ -85,15 +79,42 @@
                 for s in range(NSHIFT):
                     sel[2 * base + s, t, span, :] = slots[s]
 
+    corner = []
+    for k in range(2):
+        north, south = corner_ref[k, 0], corner_ref[k, 1]
+        north = jnp.where(top, pltpu.roll(north, HALO, 0), north)
+        south = jnp.where(bottom, pltpu.roll(south, HALO, 0), south)
+        corner.append(jnp.where(sub < HALO, south, north))
+
     for f in range(nfield):
+        place = HALO * (level * nfield + f)
+
+        def flanks(west, east):
+            west = pltpu.roll(west, LANES - HALO - place, 1)
+            east = pltpu.roll(east, lax.rem(LANES + held - place, LANES), 1)
+            return jnp.where(lane < LANES - HALO, east, west)
+
         for i in range(groups):
             span = pl.ds(SUB * i, SUB)
-            side = side_ref[f, 0, span, :]
+            side = flanks(west_ref[span, :], east_ref[span, :])
             got = [fields_ref[f, 0, span, at] for at in lanes_of]
-            got[-1] = jnp.where(lane < cols - LANES * (tiles - 1), got[-1], side)
+            got[-1] = jnp.where(lane < held, got[-1], side)
             for t, chunk in enumerate(chunked(got, side)):
                 xs[f, t, pl.ds(SUB * (i + 1), SUB), :] = chunk
-        got = [caps_ref[f, 0, :, at] for at in lanes_of]
+        got = []
+        for at in lanes_of:
+            north, south = (rows_ref[n, 0, f // 2, :, at] for n in range(2))
+            if f % 2 == 0:
+                north = pltpu.roll(north, HALO, 0)
+            else:
+                south = pltpu.roll(south, HALO, 0)
+            got.append(jnp.where(sub < HALO, south, north))
+        got[-1] = jnp.where(lane < held, got[-1], flanks(*corner))
+        for t in range(tiles):
+            back = got[t]
+            for step in (1, 2):
+                back = jnp.where((sub & step) != 0, pltpu.roll(back, step, 0), pltpu.roll(back, SUB - step, 0))
+            got[t] = jnp.where(turned, back, got[t])
         for t, chunk in enumerate(chunked(got, got[-1])):
             xs[f, t, pl.ds(0, SUB), :] = chunk
             xs[f, t, pl.ds(SUB * (groups + 1), SUB), :] = chunk
@@ -131,33 +152,127 @@
                 out_ref[f, 0, span, lanes_of[t]] = tile
 
 
+def exchange(cols, fields_ref, west_ref, east_ref, rows_ref, corner_ref, edge, ends, side, far, near, send, recv):
+    nfield, nlev, rows = fields_ref.shape[:3]
+    tiles = pl.cdiv(cols, LANES)
+    last = LANES * (tiles - 1)
+    lat_count, lon_count = lax.axis_size("lat"), lax.axis_size("lon")
+    band, sector = lax.axis_index("lat"), lax.axis_index("lon")
+    lane, sub = lane_index(), sublane_index()
+    top, bottom = band == 0, band == lat_count - 1
+    across = lax.rem(sector + lon_count // 2, lon_count)
+    up = (jnp.maximum(band - 1, 0), jnp.where(top, across, sector))
+    down = (jnp.minimum(band + 1, lat_count - 1), jnp.where(bottom, across, sector))
+    slot_up, slot_down = jnp.where(top, 0, 1), jnp.where(bottom, 1, 0)
+
+    def ahead(where, step):
+        return (where[0], lax.rem(where[1] + step + lon_count, lon_count))
+
+    here = (band, sector)
+    targets = [ahead(here, 1), ahead(here, -1)]
+    for where in (up, down):
+        targets += [where, ahead(where, 1), ahead(where, -1)]
+    barrier = pltpu.get_barrier_semaphore()
+    for target in targets:
+        pl.semaphore_signal(barrier, inc=1, device_id=target, device_id_type=pl.DeviceIdType.MESH)
+
+    for i in range(rows // SUB):
+        span = pl.ds(SUB * i, SUB)
+        packed = [jnp.zeros((SUB, LANES), jnp.float32)] * 2
+        for l in range(nlev):
+            for f in range(nfield):
+                g = HALO * (l * nfield + f)
+                mine = (lane >= g) & (lane < g + HALO)
+                ending = fields_ref[f, l, span, pl.ds(last, LANES)]
+                start = fields_ref[f, l, span, pl.ds(0, LANES)]
+                shift = (g - (cols - last - HALO)) % LANES
+                packed[0] = jnp.where(mine, pltpu.roll(ending, shift, 1) if shift else ending, packed[0])
+                packed[1] = jnp.where(mine, pltpu.roll(start, g, 1) if g else start, packed[1])
+        for k in range(2):
+            edge[k, span, :] = packed[k]
+    for l in range(nlev):
+        for j in range(nfield // 2):
+            for t in range(tiles):
+                at = pl.ds(LANES * t, LANES)
+                first = [fields_ref[2 * j + h, l, pl.ds(0, SUB), at] for h in range(2)]
+                final = [fields_ref[2 * j + h, l, pl.ds(rows - SUB, SUB), at] for h in range(2)]
+                ends[0, l, j, :, at] = jnp.where(sub < HALO, first[0], pltpu.roll(first[1], HALO, 0))
+                ends[1, l, j, :, at] = jnp.where(sub < HALO, pltpu.roll(final[0], HALO, 0), final[1])
+    pl.semaphore_wait(barrier, len(targets))
+
+    copies = []
+
+    def start_copy(source, dest, recv_sem, target):
+        copy = pltpu.make_async_remote_copy(
+            src_ref=source,
+            dst_ref=dest,
+            send_sem=send.at[len(copies)],
+            recv_sem=recv_sem,
+            device_id=target,
+            device_id_type=pl.DeviceIdType.MESH,
+        )
+        copy.start()
+        copies.append(copy)
+
+    for k, (where, slot) in enumerate(((up, slot_up), (down, slot_down))):
+        start_copy(ends.at[k], far.at[slot], recv.at[2 + slot], where)
+    for k, step in enumerate((1, -1)):
+        start_copy(edge.at[k], side.at[k], recv.at[k], ahead(here, step))
+    for n, (where, slot) in enumerate(((up, slot_up), (down, slot_down))):
+        span = pl.ds((rows - SUB) * n, SUB)
+        for k, step in enumerate((1, -1)):
+            start_copy(edge.at[k, span], near.at[k, slot], recv.at[4 + 2 * k + slot], ahead(where, step))
+    for copy in copies:
+        copy.wait_send()
+
+    def arrived(dest, sem):
+        pltpu.make_async_copy(dest, dest, recv.at[sem]).wait()
+
+    for k in range(2):
+        arrived(side.at[k], k)
+        arrived(far.at[k], 2 + k)
+        for n in range(2):
+            arrived(near.at[k, n], 4 + 2 * k + n)
+    west_ref[...] = side[0]
+    east_ref[...] = side[1]
+    corner_ref[...] = near[...]
+    rows_ref[...] = far[...]
+
+
 def halos(fields):
     nfield, nlev, rows, cols = fields.shape
-    band, lat_count, lon_count = lax.axis_index("lat"), lax.axis_size("lat"), lax.axis_size("lon")
-    west, east = beside(fields, "lon", 3, HALO, True)
-    wide = jnp.concatenate([west, fields, east], axis=3)
-    from_north, from_south = beside(wide, "lat", 2, HALO, False)
-    outgoing = jnp.where(band == 0, wide[:, :, :HALO], wide[:, :, rows - HALO :])
-    flipped = swapped(outgoing, "lon", lon_count.bit_length() - 2)[:, :, ::-1]
-    north = jnp.where(band == 0, flipped, from_north)
-    south = jnp.where(band == lat_count - 1, flipped, from_south)
-    last = LANES * ((cols - 1) // LANES)
-
-    def gap(h, n):
-        return jnp.zeros((nfield, nlev, h, n), jnp.float32)
-
-    tail = last + LANES - cols - 2 * HALO
-    side = jnp.concatenate([gap(rows, cols - last), east, gap(rows, tail), west], axis=3)
-    caps = jnp.concatenate([south, north], axis=2)
-    caps = jnp.concatenate([caps[..., HALO:], gap(2 * HALO, tail), caps[..., :HALO]], axis=3)
-    return side, caps
+    wide = pl.cdiv(cols, LANES) * LANES
+    ends = (2, nlev, nfield // 2, SUB, wide)
+    shapes = [(rows, LANES), (rows, LANES), ends, (2, 2, SUB, LANES)]
+
+    def whole(shape):
+        return pl.BlockSpec(shape, lambda n: (0,) * len(shape))
+
+    return pl.pallas_call(
+        functools.partial(exchange, cols),
+        grid=(1,),
+        out_shape=[jax.ShapeDtypeStruct(s, jnp.float32) for s in shapes],
+        in_specs=[whole((nfield, nlev, rows, wide))],
+        out_specs=[whole(s) for s in shapes],
+        scratch_shapes=[
+            pltpu.VMEM((2, rows, LANES), jnp.float32),
+            pltpu.VMEM(ends, jnp.float32),
+            pltpu.VMEM((2, rows, LANES), jnp.float32),
+            pltpu.VMEM(ends, jnp.float32),
+            pltpu.VMEM((2, 2, SUB, LANES), jnp.float32),
+            pltpu.SemaphoreType.DMA((8,)),
+            pltpu.SemaphoreType.DMA((8,)),
+        ],
+        compiler_params=pltpu.CompilerParams(collective_id=0, has_side_effects=True),
+    )(fields)
 
 
 def body(fields, dep_row, dep_col, weights):
     nfield, nlev, rows, cols = fields.shape
-    side, caps = halos(fields)
+    west, east, ends, corners = halos(fields)
     tiles = pl.cdiv(cols, LANES)
     wide = tiles * LANES
+    assert nfield % 2 == 0 and HALO * nfield * nlev <= LANES - HALO
     assert rows % SUB == 0 and CHUNK * tiles >= cols and cols + 2 * HALO <= wide
 
     def block(lead, h, w):
@@ -173,8 +288,10 @@
             point,
             point,
             block(8, rows, wide),
-            block(nfield, rows, LANES),
-            block(nfield, 2 * HALO, wide),
+            pl.BlockSpec((rows, LANES), lambda l: (0, 0)),
+            pl.BlockSpec((rows, LANES), lambda l: (0, 0)),
+            pl.BlockSpec((2, 1, nfield // 2, SUB, wide), lambda l: (0, l, 0, 0, 0)),
+            pl.BlockSpec((2, 2, SUB, LANES), lambda l: (0, 0, 0, 0)),
         ],
         out_specs=block(nfield, rows, wide),
         scratch_shapes=[
@@ -182,7 +299,7 @@
             pltpu.VMEM((2 * NSHIFT, tiles, rows, LANES), jnp.float32),
             pltpu.VMEM((nfield, tiles, rows, LANES), jnp.float32),
         ],
-    )(fields, dep_row, dep_col, weights, side, caps)
+    )(fields, dep_row, dep_col, weights, west, east, ends, corners)
 
 
 def solution(mesh):

time: 50.5 us -> 37.8 us (0.75)
  the two profiles are of different devices: /device:TPU:3 before, /device:TPU:0 now
where the time goes in v2:
time: 37.8 us; the launch traced here: 37.7 us
  Pallas kernels  37.7 us (100%)
    pallas_call x1, Pallas kernels, body(): pl.pallas_call(functools.partial(stencil, cols, cols * lax.axis_size('lon...  24.5 us
    pallas_call x1, Pallas kernels, halos(): pl.pallas_call(functools.partial(exchange, cols), grid=(1,), out_shape=[j...  13.2 us

profile of v2, /device:TPU:0, one launch (start us, length us, event | category | flops | bytes accessed | tf_op | source)
XLA Modules:
  0.0 37.7 jit_solution(13309780147429893744)
XLA Ops:
  0.0 13.2 %shard_map.46 = (f32[32,128]{1,0:T(8,128)}, f32[32,128]{1,0:T(8,128)}, f32[2,6,2,8,384]{4,3,2,1,0:T(8,128)}, f32[2,2,8,128]{3,2,1,0:T(8,128)}) custom-call(f32[4,6,32,320]{3,2,1,0:T(8,128)} %fields_ref.3), custom_call_target="tpu_custom_call" | custom-call | tf_op jit(solution)/shard_map/pallas_call | solution.py:251
  13.2 24.5 %shard_map.47 = f32[4,6,32,320]{3,2,1,0:T(8,128)} custom-call(f32[4,6,32,320]{3,2,1,0:T(8,128)} %fields_ref.3, s32[6,32,320]{2,1,0:T(8,128)} %row_ref.1, s32[6,32,320]{2,1,0:T(8,128)} %col_ref.1, f32[8,6,32,320]{3,2,1,0:T(8,128)} %weight_ref.1, f32[32,128]{1,0:T(8,128)} %get-tuple-element.9.west_ref, f32[32,128]{1,0:T(8,128)} %get-tuple-element.10.east_ref, ...), custom_call_target="tpu_custom_call" | custom-call | tf_op jit(solution)/shard_map/pallas_call | solution.py:282

commit v3 on v2

--- a/solution.py
+++ b/solution.py
@@ -50,13 +50,12 @@
     return [jnp.where(four, a, b) for a, b in zip([zero] * 4 + w, v + [zero])]
 
 
-def stencil(cols, total_cols, fields_ref, row_ref, col_ref, weight_ref, west_ref, east_ref, rows_ref, corner_ref, out_ref, xs, sel, res):
+def stencil(cols, total_cols, fields_ref, row_ref, col_ref, weight_ref, flank_ref, rows_ref, out_ref, xs, sel, res):
     nfield, rows = fields_ref.shape[0], fields_ref.shape[2]
     tiles = pl.cdiv(cols, LANES)
     groups = rows // SUB
     row0 = lax.axis_index("lat") * rows
     col0 = lax.axis_index("lon") * cols
-    level = pl.program_id(0)
     held = cols - LANES * (tiles - 1)
     lane, sub = lane_index(), sublane_index()
     top, bottom = lax.axis_index("lat") == 0, lax.axis_index("lat") == lax.axis_size("lat") - 1
@@ -79,28 +78,23 @@
                 for s in range(NSHIFT):
                     sel[2 * base + s, t, span, :] = slots[s]
 
-    corner = []
-    for k in range(2):
-        north, south = corner_ref[k, 0], corner_ref[k, 1]
-        north = jnp.where(top, pltpu.roll(north, HALO, 0), north)
-        south = jnp.where(bottom, pltpu.roll(south, HALO, 0), south)
-        corner.append(jnp.where(sub < HALO, south, north))
+    def shifted(f, t, chunk, places):
+        for s in range(NSHIFT):
+            value = chunk if s == HALO else pltpu.roll(chunk, (HALO - s) % LANES, 1)
+            for i in places:
+                xs[f, s, t, pl.ds(SUB * i, SUB), :] = value
 
     for f in range(nfield):
-        place = HALO * (level * nfield + f)
-
-        def flanks(west, east):
-            west = pltpu.roll(west, LANES - HALO - place, 1)
-            east = pltpu.roll(east, lax.rem(LANES + held - place, LANES), 1)
-            return jnp.where(lane < LANES - HALO, east, west)
+        def flanks(i):
+            return pltpu.roll(flank_ref[0, pl.ds(SUB * i, SUB), :], held - HALO * f, 1)
 
         for i in range(groups):
             span = pl.ds(SUB * i, SUB)
-            side = flanks(west_ref[span, :], east_ref[span, :])
+            side = flanks(i)
             got = [fields_ref[f, 0, span, at] for at in lanes_of]
             got[-1] = jnp.where(lane < held, got[-1], side)
             for t, chunk in enumerate(chunked(got, side)):
-                xs[f, t, pl.ds(SUB * (i + 1), SUB), :] = chunk
+                shifted(f, t, chunk, (i + 1,))
         got = []
         for at in lanes_of:
             north, south = (rows_ref[n, 0, f // 2, :, at] for n in range(2))
@@ -109,42 +103,39 @@
             else:
                 south = pltpu.roll(south, HALO, 0)
             got.append(jnp.where(sub < HALO, south, north))
-        got[-1] = jnp.where(lane < held, got[-1], flanks(*corner))
+        got[-1] = jnp.where(lane < held, got[-1], flanks(groups))
         for t in range(tiles):
             back = got[t]
             for step in (1, 2):
                 back = jnp.where((sub & step) != 0, pltpu.roll(back, step, 0), pltpu.roll(back, SUB - step, 0))
             got[t] = jnp.where(turned, back, got[t])
         for t, chunk in enumerate(chunked(got, got[-1])):
-            xs[f, t, pl.ds(0, SUB), :] = chunk
-            xs[f, t, pl.ds(SUB * (groups + 1), SUB), :] = chunk
+            shifted(f, t, chunk, (0, groups + 1))
 
     stride = rows // SUB
     many = 2 if stride % 2 == 0 else 1
     pair = 2 if nfield % 2 == 0 else 1
-    for t in range(tiles):
-        for m0 in range(0, stride, many):
-            rowsel = [
-                [sel[r, t, pl.ds(m0 + m, SUB, stride=stride), :] for r in range(NSHIFT)] for m in range(many)
-            ]
-            for f0 in range(0, nfield, pair):
-                total = [[None] * pair for _ in range(many)]
-                for s in range(NSHIFT):
-                    colsel = [sel[NSHIFT + s, t, pl.ds(m0 + m, SUB, stride=stride), :] for m in range(many)]
-                    for f in range(pair):
-                        x = []
-                        for r in range(many + NSHIFT - 1):
-                            value = xs[f0 + f, t, pl.ds(HALO + m0 + r, SUB, stride=stride), :]
-                            x.append(value if s == HALO else pltpu.roll(value, (HALO - s) % LANES, 1))
-                        for m in range(many):
-                            line = rowsel[m][0] * x[m]
-                            for r in range(1, NSHIFT):
-                                line = line + rowsel[m][r] * x[m + r]
-                            term = colsel[m] * line
-                            total[m][f] = term if s == 0 else total[m][f] + term
+    def block(n, carry):
+        f0, rest = pair * lax.rem(n, nfield // pair), n // (nfield // pair)
+        m0, t = many * lax.rem(rest, stride // many), rest // (stride // many)
+        rowsel = [[sel[r, t, pl.ds(m0 + m, SUB, stride=stride), :] for r in range(NSHIFT)] for m in range(many)]
+        total = [[None] * pair for _ in range(many)]
+        for s in range(NSHIFT):
+            colsel = [sel[NSHIFT + s, t, pl.ds(m0 + m, SUB, stride=stride), :] for m in range(many)]
+            for f in range(pair):
+                x = [xs[f0 + f, s, t, pl.ds(HALO + m0 + r, SUB, stride=stride), :] for r in range(many + NSHIFT - 1)]
                 for m in range(many):
-                    for f in range(pair):
-                        res[f0 + f, t, pl.ds(m0 + m, SUB, stride=stride), :] = total[m][f]
+                    line = rowsel[m][0] * x[m]
+                    for r in range(1, NSHIFT):
+                        line = line + rowsel[m][r] * x[m + r]
+                    term = colsel[m] * line
+                    total[m][f] = term if s == 0 else total[m][f] + term
+        for m in range(many):
+            for f in range(pair):
+                res[f0 + f, t, pl.ds(m0 + m, SUB, stride=stride), :] = total[m][f]
+        return carry
+
+    lax.fori_loop(0, tiles * (stride // many) * (nfield // pair), block, 0)
     for f in range(nfield):
         for i in range(groups):
             span = pl.ds(SUB * i, SUB)
@@ -152,7 +143,7 @@
                 out_ref[f, 0, span, lanes_of[t]] = tile
 
 
-def exchange(cols, fields_ref, west_ref, east_ref, rows_ref, corner_ref, edge, ends, side, far, near, send, recv):
+def exchange(cols, fields_ref, flank_ref, rows_ref, edge, ends, side, far, near, send, recv):
     nfield, nlev, rows = fields_ref.shape[:3]
     tiles = pl.cdiv(cols, LANES)
     last = LANES * (tiles - 1)
@@ -233,9 +224,20 @@
         arrived(far.at[k], 2 + k)
         for n in range(2):
             arrived(near.at[k, n], 4 + 2 * k + n)
-    west_ref[...] = side[0]
-    east_ref[...] = side[1]
-    corner_ref[...] = near[...]
+    gap = LANES - HALO - (cols - last)
+    corner = []
+    for k in range(2):
+        north, south = near[k, 0], near[k, 1]
+        north = jnp.where(top, pltpu.roll(north, HALO, 0), north)
+        south = jnp.where(bottom, pltpu.roll(south, HALO, 0), south)
+        corner.append(jnp.where(sub < HALO, south, north))
+    for i in range(rows // SUB + 1):
+        span = pl.ds(SUB * i, SUB)
+        west, east = (side[k, span, :] if i < rows // SUB else corner[k] for k in range(2))
+        for l in range(nlev):
+            place = HALO * nfield * l
+            moved = pltpu.roll(west, (gap - place) % LANES, 1)
+            flank_ref[l, span, :] = jnp.where(lane < gap, pltpu.roll(east, LANES - place, 1) if l else east, moved)
     rows_ref[...] = far[...]
 
 
@@ -243,7 +245,7 @@
     nfield, nlev, rows, cols = fields.shape
     wide = pl.cdiv(cols, LANES) * LANES
     ends = (2, nlev, nfield // 2, SUB, wide)
-    shapes = [(rows, LANES), (rows, LANES), ends, (2, 2, SUB, LANES)]
+    shapes = [(nlev, rows + SUB, LANES), ends]
 
     def whole(shape):
         return pl.BlockSpec(shape, lambda n: (0,) * len(shape))
@@ -269,7 +271,7 @@
 
 def body(fields, dep_row, dep_col, weights):
     nfield, nlev, rows, cols = fields.shape
-    west, east, ends, corners = halos(fields)
+    flank, ends = halos(fields)
     tiles = pl.cdiv(cols, LANES)
     wide = tiles * LANES
     assert nfield % 2 == 0 and HALO * nfield * nlev <= LANES - HALO
@@ -288,18 +290,16 @@
             point,
             point,
             block(8, rows, wide),
-            pl.BlockSpec((rows, LANES), lambda l: (0, 0)),
-            pl.BlockSpec((rows, LANES), lambda l: (0, 0)),
+            pl.BlockSpec((1, rows + SUB, LANES), lambda l: (l, 0, 0)),
             pl.BlockSpec((2, 1, nfield // 2, SUB, wide), lambda l: (0, l, 0, 0, 0)),
-            pl.BlockSpec((2, 2, SUB, LANES), lambda l: (0, 0, 0, 0)),
         ],
         out_specs=block(nfield, rows, wide),
         scratch_shapes=[
-            pltpu.VMEM((nfield, tiles, rows + 2 * SUB, LANES), jnp.float32),
+            pltpu.VMEM((nfield, NSHIFT, tiles, rows + 2 * SUB, LANES), jnp.float32),
             pltpu.VMEM((2 * NSHIFT, tiles, rows, LANES), jnp.float32),
             pltpu.VMEM((nfield, tiles, rows, LANES), jnp.float32),
         ],
-    )(fields, dep_row, dep_col, weights, west, east, ends, corners)
+    )(fields, dep_row, dep_col, weights, flank, ends)
 
 
 def solution(mesh):

time: 37.8 us -> 38.8 us (1.026)
  Pallas kernels: 37.7 us -> 38.6 us
    pallas_call x1, Pallas kernels: 24.5 us -> 25.3 us  [body(): pl.pallas_call(functools.partial(stencil, cols, cols * lax.axis_size('lon...]
where the time goes in v3:
time: 38.8 us; the launch traced here: 38.6 us
  Pallas kernels  38.6 us (99%)
    pallas_call x1, Pallas kernels, body(): pl.pallas_call(functools.partial(stencil, cols, cols * lax.axis_size('lon...  25.3 us
    pallas_call x1, Pallas kernels, halos(): pl.pallas_call(functools.partial(exchange, cols), grid=(1,), out_shape=[j...  13.3 us

profile of v3, /device:TPU:0, one launch (start us, length us, event | category | flops | bytes accessed | tf_op | source)
XLA Modules:
  0.0 38.6 jit_solution(14214298857653968386)
XLA Ops:
  0.0 13.3 %shard_map.46 = (f32[6,40,128]{2,1,0:T(8,128)}, f32[2,6,2,8,384]{4,3,2,1,0:T(8,128)}) custom-call(f32[4,6,32,320]{3,2,1,0:T(8,128)} %fields_ref.3), custom_call_target="tpu_custom_call" | custom-call | tf_op jit(solution)/shard_map/pallas_call | solution.py:253
  13.3 25.3 %shard_map.47 = f32[4,6,32,320]{3,2,1,0:T(8,128)} custom-call(f32[4,6,32,320]{3,2,1,0:T(8,128)} %fields_ref.3, s32[6,32,320]{2,1,0:T(8,128)} %row_ref.1, s32[6,32,320]{2,1,0:T(8,128)} %col_ref.1, f32[8,6,32,320]{3,2,1,0:T(8,128)} %weight_ref.1, f32[6,40,128]{2,1,0:T(8,128)} %get-tuple-element.7.flank_ref, f32[2,6,2,8,384]{4,3,2,1,0:T(8,128)} %get-tuple-element.8.rows_ref), custom_call_target="tpu_custom_call" | custom-call | tf_op jit(solution)/shard_map/pallas_call | solution.py:284

commit v4 on v3

--- a/solution.py
+++ b/solution.py
@@ -20,6 +20,14 @@
 
 def sublane_index():
     return lax.broadcasted_iota(jnp.int32, (SUB, LANES), 0)
+
+
+def tile_of(view, t, cols):
+    width = min(LANES, cols - LANES * t)
+    value = view[:, pl.ds(LANES * t, width)]
+    if width == LANES:
+        return value
+    return jnp.concatenate([value, jnp.zeros((SUB, LANES - width), value.dtype)], axis=1)
 
 
 def chunked(tiles, side=None):
@@ -66,12 +74,12 @@
         span = pl.ds(SUB * i, SUB)
         offsets = []
         for t in range(tiles):
-            o_row = row_ref[0, span, lanes_of[t]] - (row0 + SUB * i + sub) + HALO
-            back = col_ref[0, span, lanes_of[t]] - (col0 + LANES * t + lane)
+            o_row = tile_of(row_ref.at[0, span], t, cols) - (row0 + SUB * i + sub) + HALO
+            back = tile_of(col_ref.at[0, span], t, cols) - (col0 + LANES * t + lane)
             o_col = jnp.where(back > 0, back - total_cols, back) + HALO
             offsets.append(o_row * 16 + o_col)
         offsets = chunked(offsets)
-        w = [chunked([weight_ref[q, 0, span, at] for at in lanes_of]) for q in range(8)]
+        w = [chunked([tile_of(weight_ref.at[q, 0, span], t, cols) for t in range(tiles)]) for q in range(8)]
         for t in range(tiles):
             for base, offset in ((0, offsets[t] >> 4), (4, offsets[t] & 15)):
                 slots = spread(offset, [w[base + a][t] for a in range(4)])
@@ -91,7 +99,7 @@
         for i in range(groups):
             span = pl.ds(SUB * i, SUB)
             side = flanks(i)
-            got = [fields_ref[f, 0, span, at] for at in lanes_of]
+            got = [tile_of(fields_ref.at[f, 0, span], t, cols) for t in range(tiles)]
             got[-1] = jnp.where(lane < held, got[-1], side)
             for t, chunk in enumerate(chunked(got, side)):
                 shifted(f, t, chunk, (i + 1,))
@@ -140,7 +148,8 @@
         for i in range(groups):
             span = pl.ds(SUB * i, SUB)
             for t, tile in enumerate(unchunked([res[f, t, span, :] for t in range(tiles)])):
-                out_ref[f, 0, span, lanes_of[t]] = tile
+                width = min(LANES, cols - LANES * t)
+                out_ref[f, 0, span, pl.ds(LANES * t, width)] = tile[:, :width]
 
 
 def exchange(cols, fields_ref, flank_ref, rows_ref, edge, ends, side, far, near, send, recv):
@@ -174,7 +183,7 @@
             for f in range(nfield):
                 g = HALO * (l * nfield + f)
                 mine = (lane >= g) & (lane < g + HALO)
-                ending = fields_ref[f, l, span, pl.ds(last, LANES)]
+                ending = tile_of(fields_ref.at[f, l, span], tiles - 1, cols)
                 start = fields_ref[f, l, span, pl.ds(0, LANES)]
                 shift = (g - (cols - last - HALO)) % LANES
                 packed[0] = jnp.where(mine, pltpu.roll(ending, shift, 1) if shift else ending, packed[0])
@@ -185,8 +194,8 @@
         for j in range(nfield // 2):
             for t in range(tiles):
                 at = pl.ds(LANES * t, LANES)
-                first = [fields_ref[2 * j + h, l, pl.ds(0, SUB), at] for h in range(2)]
-                final = [fields_ref[2 * j + h, l, pl.ds(rows - SUB, SUB), at] for h in range(2)]
+                first = [tile_of(fields_ref.at[2 * j + h, l, pl.ds(0, SUB)], t, cols) for h in range(2)]
+                final = [tile_of(fields_ref.at[2 * j + h, l, pl.ds(rows - SUB, SUB)], t, cols) for h in range(2)]
                 ends[0, l, j, :, at] = jnp.where(sub < HALO, first[0], pltpu.roll(first[1], HALO, 0))
                 ends[1, l, j, :, at] = jnp.where(sub < HALO, pltpu.roll(final[0], HALO, 0), final[1])
     pl.semaphore_wait(barrier, len(targets))
@@ -254,7 +263,7 @@
         functools.partial(exchange, cols),
         grid=(1,),
         out_shape=[jax.ShapeDtypeStruct(s, jnp.float32) for s in shapes],
-        in_specs=[whole((nfield, nlev, rows, wide))],
+        in_specs=[whole(fields.shape)],
         out_specs=[whole(s) for s in shapes],
         scratch_shapes=[
             pltpu.VMEM((2, rows, LANES), jnp.float32),
@@ -280,20 +289,20 @@
     def block(lead, h, w):
         return pl.BlockSpec((lead, 1, h, w), lambda l: (0, l, 0, 0))
 
-    point = pl.BlockSpec((1, rows, wide), lambda l: (l, 0, 0))
+    point = pl.BlockSpec((1, rows, cols), lambda l: (l, 0, 0))
     return pl.pallas_call(
         functools.partial(stencil, cols, cols * lax.axis_size("lon")),
         grid=(nlev,),
         out_shape=jax.ShapeDtypeStruct(fields.shape, jnp.float32),
         in_specs=[
-            block(nfield, rows, wide),
+            block(nfield, rows, cols),
             point,
             point,
-            block(8, rows, wide),
+            block(8, rows, cols),
             pl.BlockSpec((1, rows + SUB, LANES), lambda l: (l, 0, 0)),
             pl.BlockSpec((2, 1, nfield // 2, SUB, wide), lambda l: (0, l, 0, 0, 0)),
         ],
-        out_specs=block(nfield, rows, wide),
+        out_specs=block(nfield, rows, cols),
         scratch_shapes=[
             pltpu.VMEM((nfield, NSHIFT, tiles, rows + 2 * SUB, LANES), jnp.float32),
             pltpu.VMEM((2 * NSHIFT, tiles, rows, LANES), jnp.float32),

time: 38.8 us -> 38.8 us (level)
  no operation moved by 1% of the time
where the time goes in v4:
time: 38.8 us; the launch traced here: 38.6 us
  Pallas kernels  38.6 us (99%)
    pallas_call x1, Pallas kernels, body(): pl.pallas_call(functools.partial(stencil, cols, cols * lax.axis_size('lon...  25.3 us
    pallas_call x1, Pallas kernels, halos(): pl.pallas_call(functools.partial(exchange, cols), grid=(1,), out_shape=[j...  13.3 us

profile of v4, /device:TPU:0, one launch (start us, length us, event | category | flops | bytes accessed | tf_op | source)
XLA Modules:
  0.0 38.6 jit_solution(14198111342365715788)
XLA Ops:
  0.0 13.3 %shard_map.46 = (f32[6,40,128]{2,1,0:T(8,128)}, f32[2,6,2,8,384]{4,3,2,1,0:T(8,128)}) custom-call(f32[4,6,32,320]{3,2,1,0:T(8,128)} %fields_ref.3), custom_call_target="tpu_custom_call" | custom-call | tf_op jit(solution)/shard_map/pallas_call | solution.py:262
  13.3 25.3 %shard_map.47 = f32[4,6,32,320]{3,2,1,0:T(8,128)} custom-call(f32[4,6,32,320]{3,2,1,0:T(8,128)} %fields_ref.3, s32[6,32,320]{2,1,0:T(8,128)} %row_ref.1, s32[6,32,320]{2,1,0:T(8,128)} %col_ref.1, f32[8,6,32,320]{3,2,1,0:T(8,128)} %weight_ref.1, f32[6,40,128]{2,1,0:T(8,128)} %get-tuple-element.7.flank_ref, f32[2,6,2,8,384]{4,3,2,1,0:T(8,128)} %get-tuple-element.8.rows_ref), custom_call_target="tpu_custom_call" | custom-call | tf_op jit(solution)/shard_map/pallas_call | solution.py:293

commit v5 on v4

--- a/solution.py
+++ b/solution.py
@@ -274,7 +274,8 @@
             pltpu.SemaphoreType.DMA((8,)),
             pltpu.SemaphoreType.DMA((8,)),
         ],
-        compiler_params=pltpu.CompilerParams(collective_id=0, has_side_effects=True),
+        cost_estimate=pl.CostEstimate(flops=0, bytes_accessed=40_000_000, transcendentals=0),
+        compiler_params=pltpu.CompilerParams(collective_id=0, has_side_effects=True, vmem_limit_bytes=16 << 20),
     )(fields)
 
 

time: 38.8 us -> 39.4 us (1.015)
  local copies, waits for them, and re-layouts: 0 us -> 2.61 us
  Pallas kernels: 38.6 us -> 36.6 us
    unnamed x0 -> x6, local copies, waits for them, and re-layouts: none -> 2.61 us
    pallas_call x1, Pallas kernels: 13.3 us -> 11.3 us  [halos(): pl.pallas_call(functools.partial(exchange, cols), grid=(1,), out_shape=[j...]
where the time goes in v5:
time: 39.4 us; the launch traced here: 39.3 us
  Pallas kernels  36.6 us (93%)
  local copies, waits for them, and re-layouts  2.61 us (7%)
    pallas_call x1, Pallas kernels, body(): pl.pallas_call(functools.partial(stencil, cols, cols * lax.axis_size('lon...  25.3 us
    pallas_call x1, Pallas kernels, halos(): pl.pallas_call(functools.partial(exchange, cols), grid=(1,), out_shape=[j...  11.3 us
    unnamed x6, local copies, waits for them, and re-layouts  2.61 us

profile of v5, /device:TPU:0, one launch (start us, length us, event | category | flops | bytes accessed | tf_op | source)
XLA Modules:
  0.0 39.3 jit_solution(1543386975793146345)
XLA Ops:
  0.0 0.0 copy-start
  0.0 1.3 %copy-done = f32[4,6,32,320]{3,2,1,0:T(8,128)S(1)} copy-done((f32[4,6,32,320]{3,2,1,0:T(8,128)S(1)}, f32[4,6,32,320]{3,2,1,0:T(8,128)}, u32[]{:S(2)}) %copy-start) | copy-done | bytes 983064
  1.3 11.3 %shard_map.46 = (f32[6,40,128]{2,1,0:T(8,128)S(1)}, f32[2,6,2,8,384]{4,3,2,1,0:T(8,128)S(1)}) custom-call(f32[4,6,32,320]{3,2,1,0:T(8,128)S(1)} %copy-done), custom_call_target="tpu_custom_call" | custom-call | bytes 40000000 | tf_op jit(solution)/shard_map/pallas_call | solution.py:262
  12.6 0.0 copy-start.1
  12.6 0.7 %copy-done.1 = f32[2,6,2,8,384]{4,3,2,1,0:T(8,128)} copy-done((f32[2,6,2,8,384]{4,3,2,1,0:T(8,128)}, f32[2,6,2,8,384]{4,3,2,1,0:T(8,128)S(1)}, u32[]{:S(2)}) %copy-start.1) | copy-done | bytes 294936
  13.3 0.0 copy-start.2
  13.3 0.6 %copy-done.2 = f32[6,40,128]{2,1,0:T(8,128)} copy-done((f32[6,40,128]{2,1,0:T(8,128)}, f32[6,40,128]{2,1,0:T(8,128)S(1)}, u32[]{:S(2)}) %copy-start.2) | copy-done | bytes 122904
  14.0 25.3 %shard_map.47 = f32[4,6,32,320]{3,2,1,0:T(8,128)} custom-call(f32[4,6,32,320]{3,2,1,0:T(8,128)} %fields_ref.3, s32[6,32,320]{2,1,0:T(8,128)} %row_ref.1, s32[6,32,320]{2,1,0:T(8,128)} %col_ref.1, f32[8,6,32,320]{3,2,1,0:T(8,128)} %weight_ref.1, f32[6,40,128]{2,1,0:T(8,128)} %copy-done.2, f32[2,6,2,8,384]{4,3,2,1,0:T(8,128)} %copy-done.1), custom_call_target="tpu_custom_call" | custom-call | tf_op jit(solution)/shard_map/pallas_call | solution.py:294
Async XLA Ops:
  0.0 1.3 %copy-start = (f32[4,6,32,320]{3,2,1,0:T(8,128)S(1)}, f32[4,6,32,320]{3,2,1,0:T(8,128)}, u32[]{:S(2)}) copy-start(f32[4,6,32,320]{3,2,1,0:T(8,128)} %fields_ref.3) | copy-start | bytes 2949124
  12.6 0.7 %copy-start.1 = (f32[2,6,2,8,384]{4,3,2,1,0:T(8,128)}, f32[2,6,2,8,384]{4,3,2,1,0:T(8,128)S(1)}, u32[]{:S(2)}) copy-start(f32[2,6,2,8,384]{4,3,2,1,0:T(8,128)S(1)} %get-tuple-element.8.rows_ref) | copy-start | bytes 884740
  13.3 0.6 %copy-start.2 = (f32[6,40,128]{2,1,0:T(8,128)}, f32[6,40,128]{2,1,0:T(8,128)S(1)}, u32[]{:S(2)}) copy-start(f32[6,40,128]{2,1,0:T(8,128)S(1)} %get-tuple-element.7.flank_ref) | copy-start | bytes 368644
